TPU v7x, 32 devices: a whole 2x2x4 slice. The times are simulated.
32 devices in a mesh: dp: 4 (over y, x), expert: 4 (over z), tensor: 2 (over core).
Axes of the slice: x: 2, y: 2, z: 4, core: 2. Of those that a mesh axis runs over, the one named last changes fastest.
Arguments:
- tokens: bfloat16 [1, 256, 3584], P(None, ('dp', 'expert'), 'tensor'), may hold values from -6 to 6
- gate_weight: bfloat16 [16, 3584, 1024], P(('dp', 'expert'), None, 'tensor'), may hold values from -0.09375 to 0.09375
- up_weight: bfloat16 [16, 3584, 1024], P(('dp', 'expert'), None, 'tensor'), may hold values from -0.09375 to 0.09375
- down_weight: bfloat16 [16, 1024, 3584], P(('dp', 'expert'), 'tensor'), may hold values from -0.1875 to 0.1875
- expert_ids: int32 [1, 256, 8], P(None, ('dp', 'expert')), may hold values from 0 to 15, all different within a row; in each aligned block of 16 rows (0 to 15, 16 to 31, ..., all dimensions but the last counted through in order) at most 16 rows name the same one
- gate_codes: int32 [1, 256, 8], P(None, ('dp', 'expert')), may hold values from 1 to 32767
Outputs:
- mixed: bfloat16 [1, 256, 3584], P(None, ('dp', 'expert'), 'tensor')
Inputs may be any that keep to these rules, and one draw needn't show every extreme that they name: `expert_ids`: the 8 experts of one token differ. For every step, of the 16 tokens that one index of dp+expert holds, no expert is named by more than 16.
All inputs are finite; a program needn't handle non-finite values.
Results may differ from a plain program's by a relative error of at most 0.0095.
Values may be sent and summed in bfloat16 or wider, within the bound.
A program may use at most 64 MiB of HBM per device.

v0:
```python
import jax
import jax.numpy as jnp
from jax import lax
from jax.sharding import PartitionSpec as P


def local(tokens, gate_weight, up_weight, down_weight, expert_ids, gate_codes):
    owners = lax.axis_size("dp") * lax.axis_size("expert")
    tok_rows = tokens.shape[1]
    top_count = expert_ids.shape[2]
    slot_depth = min(tok_rows, max(2, 2 * tok_rows * top_count // owners))
    slot_count = owners * slot_depth
    w_gate = gate_weight[0]
    w_up = up_weight[0]
    w_down = down_weight[0]
    slot_numbers = jnp.arange(slot_count, dtype=jnp.int32)
    owner_numbers = jnp.arange(owners, dtype=jnp.int32)
    step_tokens = tokens[0]
    route_ids = expert_ids[0].reshape(tok_rows * top_count)
    onehot = (route_ids[:, None] == owner_numbers[None, :]).astype(jnp.int32)
    before = jnp.cumsum(onehot, axis=0) - onehot
    slot_rank = jnp.sum(before * onehot, axis=1)
    slot_index = route_ids * slot_depth + slot_rank
    select = (slot_index[:, None] == slot_numbers[None, :]).astype(jnp.bfloat16)
    per_token = jnp.sum(select.reshape(tok_rows, top_count, slot_count), axis=1)
    packed = jnp.einsum(
        "ts,td->sd", per_token, step_tokens, preferred_element_type=jnp.float32
    ).astype(jnp.bfloat16)
    packed = packed.reshape(owners, slot_depth, step_tokens.shape[1])
    arrived = lax.all_to_all(packed, ("dp", "expert"), split_axis=0, concat_axis=0, tiled=True)
    owner_rows = arrived.reshape(slot_count, step_tokens.shape[1])
    owner_rows = lax.all_gather(owner_rows, "tensor", axis=1, tiled=True)
    gated = jnp.dot(owner_rows, w_gate, preferred_element_type=jnp.float32)
    lifted = jnp.dot(owner_rows, w_up, preferred_element_type=jnp.float32)
    hidden = (jax.nn.silu(gated) * lifted).astype(jnp.bfloat16)
    partial_value = jnp.dot(hidden, w_down, preferred_element_type=jnp.float32).astype(jnp.bfloat16)
    summed = (
        lax.psum_scatter(partial_value, "tensor", scatter_dimension=1, tiled=True)
        .astype(jnp.float32)
        .astype(jnp.bfloat16)
    )
    half_width = summed.shape[1]
    result = summed.reshape(owners, slot_depth, half_width)
    returned = lax.all_to_all(result, ("dp", "expert"), split_axis=0, concat_axis=0, tiled=True)
    returned = returned.reshape(slot_count, half_width)
    picked = jnp.dot(select, returned, preferred_element_type=jnp.float32)
    codes = gate_codes[0].astype(jnp.float32)
    shares = codes / jnp.sum(codes, axis=1, keepdims=True)
    mixed_rows = jnp.sum(
        picked.reshape(tok_rows, top_count, half_width) * shares[:, :, None], axis=1
    )
    outputs = [mixed_rows.astype(jnp.bfloat16)]
    return jnp.stack(outputs)


def solution(mesh):
    in_specs = (
        P(None, ("dp", "expert"), "tensor"),
        P(("dp", "expert"), None, "tensor"),
        P(("dp", "expert"), None, "tensor"),
        P(("dp", "expert"), "tensor", None),
        P(None, ("dp", "expert"), None),
        P(None, ("dp", "expert"), None),
    )
    out_specs = P(None, ("dp", "expert"), "tensor")
    return jax.shard_map(local, mesh=mesh, in_specs=in_specs, out_specs=out_specs, check_vma=False)
```

profile of v0, /device:TPU:0, one launch (start us, length us, event | category | flops | bytes accessed | tf_op | source)
XLA Modules:
  0.0 110.7 jit_solution(10478560798243014809)
XLA Ops:
  6.5 0.0 copy-start
  6.5 0.0 all-gather.2.cloned.1.call-start
  6.5 0.8 copy.17
  7.3 0.1 eq.51
  7.4 0.1 fusion.25
  7.5 0.2 reduce_window_sum.11
  7.7 0.2 select_reduce_fusion
  7.8 0.1 reduce_sum.42
  7.9 0.1 copy.18
  8.0 0.7 bitcast_add_fusion
  8.7 0.1 copy.19
  8.8 0.1 fusion.23
  8.9 0.0 copy-done
  8.9 0.4 convolution_convert_fusion.1
  9.3 32.9 %all_to_all.10 = bf16[16,16,1792]{2,1,0:T(8,128)(2,1)} all-to-all(bf16[16,16,1792]{2,1,0:T(8,128)(2,1)S(1)} %bitcast.39), channel_id=1, replica_groups=mesh['dp'=4,'expert'=4,'tensor'=2] {'dp','expert'}, dimensions={0} | all-to-all | bytes 1835008 | tf_op jit(solution)/shard_map/all_to_all | solution.py:30
  42.2 0.0 all-gather.2.cloned.1.call-update
  42.2 0.0 reduce-scatter.2.cloned.1.call-start
  42.3 7.5 %all-gather.2.cloned.1.call-done = bf16[256,3584]{1,0:T(8,128)(2,1)} async-done(((bf16[256,1792]{1,0:T(8,128)(2,1)}), bf16[256,3584]{1,0:T(8,128)(2,1)}) %all-gather.2.cloned.1.call-update) | async-done | bytes 1835024 | tf_op jit(solution)/shard_map/all_gather | solution.py:32
  49.8 0.0 copy-start.2
  49.8 3.8 %fusion.3 = f32[256,512]{1,0:T(8,128)S(1)} fusion(bf16[256,3584]{1,0:T(8,128)(2,1)} %all-gather.2.cloned.1.call-done, bf16[1,3584,512]{2,1,0:T(8,128)(2,1)} %param.7), kind=kOutput, calls=%fused_computation.4 | convolution fusion | flops 939524096 | bytes 6029312 | tf_op jit(solution)/shard_map/dot_general | solution.py:33
  53.6 0.0 copy-done.2
  53.7 6.6 %convolution_convert_fusion = bf16[256,3584]{1,0:T(8,128)(2,1)} fusion(bf16[1,512,3584]{2,1,0:T(8,128)(2,1)} %param.9, bf16[256,3584]{1,0:T(8,128)(2,1)S(1)} %copy-done.2, bf16[1,3584,512]{2,1,0:T(8,128)(2,1)} %param.8, f32[256,512]{1,0:T(8,128)S(1)} %fusion.3), kind=kOutput, calls=%fused_computation | convolution fusion | flops 1880752128 | bytes 11534336 | tf_op jit(solution)/shard_map/dot_general | solution.py:36
  60.2 0.0 copy-start.1
  60.2 0.0 reduce-scatter.2.cloned.1.call-update
  60.2 10.6 %reduce-scatter.2.cloned.1.call-done = bf16[256,1792]{1,0:T(8,128)(2,1)} async-done(((bf16[256,3584]{1,0:T(8,128)(2,1)}), bf16[256,1792]{1,0:T(8,128)(2,1)}) %reduce-scatter.2.cloned.1.call-update) | async-done | bytes 917520 | tf_op jit(solution)/shard_map/reduce_scatter | solution.py:38
  70.9 6.9 %all-to-all-start.1 = ((bf16[16,16,1792]{2,1,0:T(8,128)(2,1)}), bf16[16,16,1792]{2,1,0:T(8,128)(2,1)S(1)}, u32[]{:S(2)}, u32[]{:S(2)}) async-start(bf16[16,16,1792]{2,1,0:T(8,128)(2,1)} %bitcast.40), calls=%async_computation.2 | async-start | bytes 1835008 | tf_op jit(solution)/shard_map/all_to_all | solution.py:44
  77.8 0.0 copy-done.1
  77.8 0.1 copy.21
  77.9 24.9 %all-to-all-done.1 = bf16[16,16,1792]{2,1,0:T(8,128)(2,1)S(1)} async-done(((bf16[16,16,1792]{2,1,0:T(8,128)(2,1)}), bf16[16,16,1792]{2,1,0:T(8,128)(2,1)S(1)}, u32[]{:S(2)}, u32[]{:S(2)}) %all-to-all-start.1) | async-done | bytes 917536 | tf_op jit(solution)/shard_map/all_to_all | solution.py:44
  102.8 1.1 fusion.8
  (2 shorter events, 0.0 us)
Async XLA Ops:
  6.5 2.4 %copy-start = (bf16[1,16,1792]{2,1,0:T(8,128)(2,1)S(1)}, bf16[1,16,1792]{2,1,0:T(8,128)(2,1)}, u32[]{:S(2)}) copy-start(bf16[1,16,1792]{2,1,0:T(8,128)(2,1)} %param.6) | copy-start | bytes 172036
  6.5 43.3 %all-gather.2.cloned.1.call-start = ((), (), s32[]{:S(2)}) async-start(), calls=%async_computation.3 | async-start | bytes 2752512 | tf_op jit(solution)/shard_map/all_gather | solution.py:32
  42.2 28.6 %reduce-scatter.2.cloned.1.call-start = ((), (), s32[]{:S(2)}) async-start(), calls=%async_computation.4 | async-start | bytes 2752512 | tf_op jit(solution)/shard_map/reduce_scatter | solution.py:38
  49.8 3.8 %copy-start.2 = (bf16[256,3584]{1,0:T(8,128)(2,1)S(1)}, bf16[256,3584]{1,0:T(8,128)(2,1)}, u32[]{:S(2)}) copy-start(bf16[256,3584]{1,0:T(8,128)(2,1)} %all-gather.2.cloned.1.call-done) | copy-start | bytes 5505028
  60.2 17.6 %copy-start.1 = (s32[1,16,8]{1,2,0:T(8,128)S(1)}, s32[1,16,8]{1,2,0:T(8,128)}, u32[]{:S(2)}) copy-start(s32[1,16,8]{1,2,0:T(8,128)} %param.11) | copy-start | bytes 1540
  70.9 31.9 %all-to-all-start.1 = ((bf16[16,16,1792]{2,1,0:T(8,128)(2,1)}), bf16[16,16,1792]{2,1,0:T(8,128)(2,1)S(1)}, u32[]{:S(2)}, u32[]{:S(2)}) async-start(bf16[16,16,1792]{2,1,0:T(8,128)(2,1)} %bitcast.40), calls=%async_computation.2 | async-start | bytes 1835008 | tf_op jit(solution)/shard_map/all_to_all | solution.py:44
Sparse Core Ops, SparseCore 0:
  42.4 7.3 all-gather.1
  60.4 10.4 reduce-scatter.1
where the time goes:
time: 111 us
  waiting for transfers between devices  43 us (39%)
  blocking collectives  32.9 us (30%)
  between operations  13.5 us (12%)
  matrix products  11.9 us (11%)
  starting transfers between devices  6.97 us (6%)
  other arithmetic  1.28 us (1%)
  local copies, waits for them, and re-layouts  1.18 us (1%)
    all_to_all x1, blocking collectives, local(): lax.all_to_all(packed, ('dp', 'expert'), split_axis=0, concat_axis=0, til...  32.9 us
    all_to_all x1, waiting for transfers between devices, local(): lax.all_to_all(result, ('dp', 'expert'), split_axis=0, concat_axis=0, til...  24.9 us
    reduce_scatter x1, waiting for transfers between devices, local(): lax.psum_scatter(partial_value, 'tensor', scatter_dimension=1, tiled=True)  10.6 us
    all_gather x1, waiting for transfers between devices, local(): owner_rows = lax.all_gather(owner_rows, 'tensor', axis=1, tiled=True)  7.52 us
    all_to_all x1, starting transfers between devices, local(): lax.all_to_all(result, ('dp', 'expert'), split_axis=0, concat_axis=0, til...  6.92 us
    dot_general x1, matrix products, local(): jnp.dot(hidden, w_down, preferred_element_type=jnp.float32)  6.57 us
    dot_general x1, matrix products, local(): gated = jnp.dot(owner_rows, w_gate, preferred_element_type=jnp.float32)  3.82 us
  transfers between devices with their start and end apart: 3, of which 3 were waited for; matrix products, arithmetic and copies ran while one was open for 0% of the time, Pallas kernels for 0%

commit v1 on v0

--- a/solution.py
+++ b/solution.py
@@ -1,7 +1,223 @@
+import functools
 import jax
 import jax.numpy as jnp
 from jax import lax
+from jax.experimental import pallas as pl
+from jax.experimental.pallas import tpu as pltpu
 from jax.sharding import PartitionSpec as P
+
+MESH = pl.DeviceIdType.MESH
+LANES = 128
+ORDER = (
+    "F10", "F11", "F20", "F12", "F21", "F30", "F13", "F22", "F31", "C0", "F23", "F32", "C1", "R10",
+    "F33", "C2", "R11", "R20", "C3", "R12", "R21", "R30", "R13", "R22", "R31", "R23", "R32", "R33",
+)
+
+
+def exchange_kernel(
+    owners, layers, tokens_ref, ids_ref, codes_ref, gate_ref, up_ref, down_ref, out_ref,
+    rows, w_gate, w_up, w_down, part_own, part_send, part_recv,
+    b_send, b_recv, a_send, a_recv, z_send, z_recv, weight_sem,
+    gz_s, gz_r, ga_s, ga_r, gb_s, gb_r, gc_s, gc_r,
+    rp_s, rp_r, rb_s, rb_r, ra_s, ra_r, rz_s, rz_r,
+):
+    tok, half = tokens_ref.shape[1], tokens_ref.shape[2]
+    dp, z, core = lax.axis_index("dp"), lax.axis_index("expert"), lax.axis_index("tensor")
+    expert = dp * layers + z
+    x_peer = dp + 1 - 2 * (dp % 2)
+    y_peer = (dp + 2) % 4
+    a_peer = {"dp": x_peer * (1 - core) + y_peer * core}
+    b_peer = {"dp": y_peer * (1 - core) + x_peer * core}
+    c_peer = {"tensor": 1 - core}
+    flips = [z, z + 1 - 2 * (z % 2), (z + 2) % 4, 3 - z]
+    z_peer = [{"expert": flip} for flip in flips]
+
+    loads = []
+    for side in range(2):
+        first = pl.multiple_of((core if side == 0 else 1 - core) * half, LANES)
+        loads.append(pltpu.make_async_copy(gate_ref.at[0, pl.ds(first, half), :], w_gate.at[side], weight_sem.at[side, 0]))
+        loads.append(pltpu.make_async_copy(up_ref.at[0, pl.ds(first, half), :], w_up.at[side], weight_sem.at[side, 1]))
+    for side in range(2):
+        first = pl.multiple_of((core if side == 0 else 1 - core) * half, LANES)
+        loads.append(pltpu.make_async_copy(down_ref.at[0, :, pl.ds(first, half)], w_down.at[side], weight_sem.at[side, 2]))
+    for load in loads:
+        load.start()
+
+    barrier = pltpu.get_barrier_semaphore()
+    peers = [a_peer, b_peer, c_peer] + z_peer[1:]
+    for peer in peers:
+        pl.semaphore_signal(barrier, inc=1, device_id=peer, device_id_type=MESH)
+
+    rows[0, 0, 0:tok, 0:half] = tokens_ref[0]
+    codes = codes_ref[0].astype(jnp.float32)
+    share = codes / jnp.sum(codes, axis=1, keepdims=True)
+    ids = ids_ref[0]
+    lane = lax.broadcasted_iota(jnp.int32, (tok, LANES), 1)
+    packed = jnp.zeros((tok, LANES), jnp.float32)
+    rest = share
+    for term in range(3):
+        rounded = rest.astype(jnp.bfloat16).astype(jnp.float32)
+        rest = rest - rounded
+        for k in range(ids.shape[1]):
+            packed = jnp.where(lane == ids[:, k:k + 1] + term * owners, rounded[:, k:k + 1], packed)
+    rows[0, 0, 0:tok, half:half + LANES] = packed.astype(jnp.bfloat16)
+    pl.semaphore_wait(barrier, len(peers))
+
+    def remote(src, dst, send, recv, peer):
+        return pltpu.make_async_remote_copy(
+            src_ref=src, dst_ref=dst, send_sem=send, recv_sem=recv, device_id=peer, device_id_type=MESH
+        )
+
+    def block(layer, side, spot, count=1, wide=True):
+        view = rows.at[layer, side, spot * tok:(spot + count) * tok]
+        return view if wide else rows.at[layer, side, spot * tok:(spot + count) * tok, 0:half]
+
+    sent = []
+
+    def send(copy):
+        copy.start()
+        sent.append(copy)
+
+    gather_z = [None] + [
+        remote(block(0, 0, 0), block(i, 0, 0), gz_s.at[i], gz_r.at[i], z_peer[i]) for i in range(1, layers)
+    ]
+    gather_a = [remote(block(i, 0, 0), block(i, 0, 1), ga_s.at[i], ga_r.at[i], a_peer) for i in range(layers)]
+    gather_b = [
+        [remote(block(i, 0, s), block(i, 0, 2 + s), gb_s.at[i, s], gb_r.at[i, s], b_peer) for s in range(2)]
+        for i in range(layers)
+    ]
+    swap = (0, 2, 1, 3)
+    gather_c = [
+        [
+            remote(block(i, 0, s, wide=False), block(i, 1, swap[s], wide=False), gc_s.at[i, swap[s]], gc_r.at[i, swap[s]], c_peer)
+            for s in range(4)
+        ]
+        for i in range(layers)
+    ]
+    reduce_p = [remote(part_send.at[i], part_recv.at[i], rp_s.at[i], rp_r.at[i], c_peer) for i in range(layers)]
+    reduce_b = [remote(b_send.at[i], b_recv.at[i], rb_s.at[i], rb_r.at[i], b_peer) for i in range(layers)]
+    reduce_a = [remote(a_send.at[i], a_recv.at[i], ra_s.at[i], ra_r.at[i], a_peer) for i in range(layers)]
+    reduce_z = [None] + [
+        remote(z_send.at[i], z_recv.at[i], rz_s.at[i], rz_r.at[i], z_peer[i]) for i in range(1, layers)
+    ]
+    kept = [None] * layers
+    loaded = []
+
+    def first_hop(i):
+        if i == 0:
+            for j in range(1, layers):
+                send(gather_z[j])
+        else:
+            gather_z[i].wait_recv()
+        send(gather_a[i])
+        send(gather_b[i][0])
+        send(gather_c[i][0])
+
+    def second_hop(i):
+        gather_a[i].wait_recv()
+        send(gather_b[i][1])
+        send(gather_c[i][1])
+
+    def third_hop(i):
+        for s in range(2):
+            gather_b[i][s].wait_recv()
+            send(gather_c[i][2 + s])
+
+    def compute(i):
+        for s in range(4):
+            gather_c[i][s].wait_recv()
+        if not loaded:
+            for load in loads:
+                load.wait()
+            loaded.append(True)
+        own, other = rows[i, 0, :, 0:half], rows[i, 1, :, 0:half]
+        dot = functools.partial(jnp.dot, preferred_element_type=jnp.float32)
+        gated = dot(own, w_gate[0]) + dot(other, w_gate[1])
+        lifted = dot(own, w_up[0]) + dot(other, w_up[1])
+        hidden = (gated / (1.0 + jnp.exp(-gated)) * lifted).astype(jnp.bfloat16)
+        away = dot(hidden, w_down[1]).astype(jnp.bfloat16)
+        for s in range(4):
+            part_send[i, swap[s] * tok:(swap[s] + 1) * tok, :] = away[s * tok:(s + 1) * tok]
+        send(reduce_p[i])
+        part_own[i] = dot(hidden, w_down[0]).astype(jnp.bfloat16)
+
+    def first_sum(i):
+        reduce_p[i].wait_recv()
+        names = rows[i, 0, :, half:half + LANES].astype(jnp.float32)
+        spots = lax.broadcasted_iota(jnp.int32, names.shape, 1)
+        mine = (spots == expert) | (spots == expert + owners) | (spots == expert + 2 * owners)
+        weight = jnp.sum(jnp.where(mine, names, 0.0), axis=1, keepdims=True)
+        total = (part_own[i].astype(jnp.float32) + part_recv[i].astype(jnp.float32)) * weight
+        b_send[i] = total[2 * tok:].astype(jnp.bfloat16)
+        send(reduce_b[i])
+        part_own[i, 0:2 * tok, :] = total[0:2 * tok].astype(jnp.bfloat16)
+
+    def second_sum(i):
+        reduce_b[i].wait_recv()
+        total = part_own[i, 0:2 * tok, :].astype(jnp.float32) + b_recv[i].astype(jnp.float32)
+        a_send[i] = total[tok:].astype(jnp.bfloat16)
+        send(reduce_a[i])
+        part_own[i, 0:tok, :] = total[0:tok].astype(jnp.bfloat16)
+
+    def third_sum(i):
+        reduce_a[i].wait_recv()
+        total = part_own[i, 0:tok, :].astype(jnp.float32) + a_recv[i].astype(jnp.float32)
+        if i == 0:
+            part_own[i, 0:tok, :] = total.astype(jnp.bfloat16)
+        else:
+            z_send[i] = total.astype(jnp.bfloat16)
+            send(reduce_z[i])
+
+    stages = {"F1": first_hop, "F2": second_hop, "F3": third_hop, "R1": first_sum, "R2": second_sum, "R3": third_sum, "C": compute}
+    for name in ORDER:
+        stages[name[:-1]](int(name[-1]))
+
+    total = part_own[0, 0:tok, :].astype(jnp.float32)
+    for i in range(1, layers):
+        reduce_z[i].wait_recv()
+        total = total + z_recv[i].astype(jnp.float32)
+    out_ref[0] = total.astype(out_ref.dtype)
+    for copy in sent:
+        copy.wait_send()
+
+
+def exchange(tokens, gate_weight, up_weight, down_weight, expert_ids, gate_codes):
+    layers = lax.axis_size("expert")
+    owners = lax.axis_size("dp") * layers
+    _, tok, half = tokens.shape
+    columns = owners // layers
+    units = gate_weight.shape[2]
+    vmem, hbm = pl.BlockSpec(memory_space=pltpu.VMEM), pl.BlockSpec(memory_space=pl.ANY)
+    dma = pltpu.SemaphoreType.DMA
+    bf16 = jnp.bfloat16
+    pair = (pltpu.VMEM((layers, tok, half), bf16),) * 2
+    return pl.pallas_call(
+        functools.partial(exchange_kernel, owners, layers),
+        out_shape=jax.ShapeDtypeStruct(tokens.shape, tokens.dtype),
+        in_specs=[vmem] * 3 + [hbm] * 3,
+        out_specs=vmem,
+        scratch_shapes=[
+            pltpu.VMEM((layers, 2, columns * tok, half + LANES), bf16),
+            pltpu.VMEM((2, half, units), bf16),
+            pltpu.VMEM((2, half, units), bf16),
+            pltpu.VMEM((2, units, half), bf16),
+            pltpu.VMEM((layers, columns * tok, half), bf16),
+            pltpu.VMEM((layers, columns * tok, half), bf16),
+            pltpu.VMEM((layers, columns * tok, half), bf16),
+            pltpu.VMEM((layers, 2 * tok, half), bf16),
+            pltpu.VMEM((layers, 2 * tok, half), bf16),
+            *pair, *pair,
+            dma((2, 3)),
+            dma((layers,)), dma((layers,)),
+            dma((layers,)), dma((layers,)),
+            dma((layers, 2)), dma((layers, 2)),
+            dma((layers, 4)), dma((layers, 4)),
+            *([dma((layers,))] * 8),
+        ],
+        compiler_params=pltpu.CompilerParams(
+            collective_id=0, has_side_effects=True, vmem_limit_bytes=48 * 1024 * 1024
+        ),
+    )(tokens, expert_ids, gate_codes, gate_weight, up_weight, down_weight)
 
 
 def local(tokens, gate_weight, up_weight, down_weight, expert_ids, gate_codes):
@@ -9,6 +225,11 @@
     tok_rows = tokens.shape[1]
     top_count = expert_ids.shape[2]
     slot_depth = min(tok_rows, max(2, 2 * tok_rows * top_count // owners))
+    if (
+        slot_depth == tok_rows and lax.axis_size("dp") == 4 and lax.axis_size("expert") == 4
+        and lax.axis_size("tensor") == 2 and tokens.shape[0] == 1 and tok_rows % 16 == 0
+    ):
+        return exchange(tokens, gate_weight, up_weight, down_weight, expert_ids, gate_codes)
     slot_count = owners * slot_depth
     w_gate = gate_weight[0]
     w_up = up_weight[0]

time: 111 us -> 46.1 us (0.42)
  waiting for transfers between devices: 43 us -> 0 us
  Pallas kernels: 0 us -> 40.9 us
  blocking collectives: 32.9 us -> 0 us
  between operations: 13.5 us -> 0.01 us
  matrix products: 11.9 us -> 0 us
  starting transfers between devices: 6.97 us -> 0 us
  local copies, waits for them, and re-layouts: 1.18 us -> 5 us
  other arithmetic: 1.28 us -> 0 us
    pallas_call x0 -> x1, Pallas kernels: none -> 40.9 us  [exchange(): pl.pallas_call(functools.partial(exchange_kernel, owners, layers), out_sh...]
    all_to_all x1 -> x0, blocking collectives: 32.9 us -> none  [local(): lax.all_to_all(packed, ('dp', 'expert'), split_axis=0, concat_axis=0, til...]
    all_to_all x1 -> x0, waiting for transfers between devices: 24.9 us -> none  [local(): lax.all_to_all(result, ('dp', 'expert'), split_axis=0, concat_axis=0, til...]
    dot_general x4 -> x0, matrix products: 11.9 us -> none  [the longest x1 6.57 us: local(): jnp.dot(hidden, w_down, preferred_element_type=jnp.float32)]
    reduce_scatter x1 -> x0, waiting for transfers between devices: 10.6 us -> none  [local(): lax.psum_scatter(partial_value, 'tensor', scatter_dimension=1, tiled=True)]
    all_gather x1 -> x0, waiting for transfers between devices: 7.52 us -> none  [local(): owner_rows = lax.all_gather(owner_rows, 'tensor', axis=1, tiled=True)]
    all_to_all x1 -> x0, starting transfers between devices: 6.92 us -> none  [local(): lax.all_to_all(result, ('dp', 'expert'), split_axis=0, concat_axis=0, til...]
    unnamed x7, local copies, waits for them, and re-layouts: 0.78 us -> 5 us
  transfers between devices with their start and end apart: 3 -> 0, of which waited for: 3 -> 0; matrix products, arithmetic and copies ran while one was open for 0% -> 0% of each run, Pallas kernels for 0% -> 0%
where the time goes in v1:
time: 46.1 us; the launch traced here: 45.9 us
  Pallas kernels  40.9 us (89%)
  local copies, waits for them, and re-layouts  5 us (11%)
    pallas_call x1, Pallas kernels, exchange(): pl.pallas_call(functools.partial(exchange_kernel, owners, layers), out_sh...  40.9 us
    unnamed x7, local copies, waits for them, and re-layouts  5 us

profile of v1, /device:TPU:0, one launch (start us, length us, event | category | flops | bytes accessed | tf_op | source)
XLA Modules:
  0.0 45.9 jit_solution(9405561076881323521)
XLA Ops:
  0.0 0.8 %copy.7.ids_ref = s32[1,16,8]{2,1,0:T(8,128)S(1)} copy(s32[1,16,8]{1,2,0:T(8,128)} %param.10) | data formatting | bytes 1024 | tf_op args[4]
  0.8 0.8 %copy.8.codes_ref = s32[1,16,8]{2,1,0:T(8,128)S(1)} copy(s32[1,16,8]{1,2,0:T(8,128)} %param.11) | data formatting | bytes 1024 | tf_op args[5]
  1.5 0.0 copy-start
  1.5 2.0 %copy-done = bf16[1,3584,512]{2,1,0:T(8,128)(2,1)S(1)} copy-done((bf16[1,3584,512]{2,1,0:T(8,128)(2,1)S(1)}, bf16[1,3584,512]{2,1,0:T(8,128)(2,1)}, u32[]{:S(2)}) %copy-start) | copy-done | bytes 3670040
  3.6 0.0 copy-start.1
  3.6 0.8 %copy-done.1 = bf16[1,16,1792]{2,1,0:T(8,128)(2,1)S(1)} copy-done((bf16[1,16,1792]{2,1,0:T(8,128)(2,1)S(1)}, bf16[1,16,1792]{2,1,0:T(8,128)(2,1)}, u32[]{:S(2)}) %copy-start.1) | copy-done | bytes 57368
  4.4 40.9 %shard_map.64 = bf16[1,16,1792]{2,1,0:T(8,128)(2,1)S(1)} custom-call(bf16[1,16,1792]{2,1,0:T(8,128)(2,1)S(1)} %copy-done.1, s32[1,16,8]{2,1,0:T(8,128)S(1)} %copy.7.ids_ref, s32[1,16,8]{2,1,0:T(8,128)S(1)} %copy.8.codes_ref, bf16[1,3584,512]{2,1,0:T(8,128)(2,1)S(1)} %copy-done, bf16[1,3584,512]{2,1,0:T(8,128)(2,1)} %up_ref.1, bf16[1,512,3584]{2,1,0:T(8,128)(2,1)} %down_ref.1), custom_call_target="tpu_custom_call" | custom-call | tf_op jit(solution)/shard_map/pallas_call | solution.py:194
  45.2 0.6 %copy.10 = bf16[1,16,1792]{2,1,0:T(8,128)(2,1)} copy(bf16[1,16,1792]{2,1,0:T(8,128)(2,1)S(1)} %shard_map.64) | data formatting | bytes 114688
Async XLA Ops:
  1.5 2.0 %copy-start = (bf16[1,3584,512]{2,1,0:T(8,128)(2,1)S(1)}, bf16[1,3584,512]{2,1,0:T(8,128)(2,1)}, u32[]{:S(2)}) copy-start(bf16[1,3584,512]{2,1,0:T(8,128)(2,1)} %gate_ref.1) | copy-start | bytes 11010052
  3.6 0.8 %copy-start.1 = (bf16[1,16,1792]{2,1,0:T(8,128)(2,1)S(1)}, bf16[1,16,1792]{2,1,0:T(8,128)(2,1)}, u32[]{:S(2)}) copy-start(bf16[1,16,1792]{2,1,0:T(8,128)(2,1)} %tokens_ref.1) | copy-start | bytes 172036

commit v2 on v1

--- a/solution.py
+++ b/solution.py
@@ -49,9 +49,9 @@
         pl.semaphore_signal(barrier, inc=1, device_id=peer, device_id_type=MESH)
 
     rows[0, 0, 0:tok, 0:half] = tokens_ref[0]
-    codes = codes_ref[0].astype(jnp.float32)
+    codes = codes_ref[0].astype(jnp.float32).T
     share = codes / jnp.sum(codes, axis=1, keepdims=True)
-    ids = ids_ref[0]
+    ids = ids_ref[0].T
     lane = lax.broadcasted_iota(jnp.int32, (tok, LANES), 1)
     packed = jnp.zeros((tok, LANES), jnp.float32)
     rest = share
@@ -215,9 +215,9 @@
             *([dma((layers,))] * 8),
         ],
         compiler_params=pltpu.CompilerParams(
-            collective_id=0, has_side_effects=True, vmem_limit_bytes=48 * 1024 * 1024
+            collective_id=0, has_side_effects=True, vmem_limit_bytes=63 * 1024 * 1024
         ),
-    )(tokens, expert_ids, gate_codes, gate_weight, up_weight, down_weight)
+    )(tokens, expert_ids.swapaxes(1, 2), gate_codes.swapaxes(1, 2), gate_weight, up_weight, down_weight)
 
 
 def local(tokens, gate_weight, up_weight, down_weight, expert_ids, gate_codes):

time: 46.1 us -> 43.7 us (0.948)
  local copies, waits for them, and re-layouts: 5 us -> 1.45 us
  Pallas kernels: 40.9 us -> 42 us
    unnamed x7 -> x1, local copies, waits for them, and re-layouts: 5 us -> 1.45 us
    pallas_call x1, Pallas kernels: 40.9 us -> 42 us  [exchange(): pl.pallas_call(functools.partial(exchange_kernel, owners, layers), out_sh...]
where the time goes in v2:
time: 43.7 us; the launch traced here: 43.5 us
  Pallas kernels  42 us (96%)
  local copies, waits for them, and re-layouts  1.45 us (3%)
    pallas_call x1, Pallas kernels, exchange(): pl.pallas_call(functools.partial(exchange_kernel, owners, layers), out_sh...  42 us
    unnamed x1, local copies, waits for them, and re-layouts  1.45 us

profile of v2, /device:TPU:0, one launch (start us, length us, event | category | flops | bytes accessed | tf_op | source)
XLA Modules:
  0.0 43.5 jit_solution(6429575669321075663)
XLA Ops:
  0.0 42.0 %shard_map.64 = bf16[1,16,1792]{2,1,0:T(8,128)(2,1)} custom-call(bf16[1,16,1792]{2,1,0:T(8,128)(2,1)} %tokens_ref.1, s32[1,8,16]{2,1,0:T(8,128)} %bitcast.2, s32[1,8,16]{2,1,0:T(8,128)} %bitcast.3, bf16[1,3584,512]{2,1,0:T(8,128)(2,1)} %gate_ref.1, bf16[1,3584,512]{2,1,0:T(8,128)(2,1)} %up_ref.1, bf16[1,512,3584]{2,1,0:T(8,128)(2,1)} %down_ref.1), custom_call_target="tpu_custom_call" | custom-call | tf_op jit(solution)/shard_map/pallas_call | solution.py:194
  42.0 1.4 %copy.8 = bf16[1,16,1792]{2,1,0:T(8,128)(2,1)} copy(bf16[1,16,1792]{2,1,0:T(8,128)(2,1)} %shard_map.64) | data formatting | bytes 114688

commit v3 on v2

--- a/solution.py
+++ b/solution.py
@@ -8,10 +8,7 @@
 
 MESH = pl.DeviceIdType.MESH
 LANES = 128
-ORDER = (
-    "F10", "F11", "F20", "F12", "F21", "F30", "F13", "F22", "F31", "C0", "F23", "F32", "C1", "R10",
-    "F33", "C2", "R11", "R20", "C3", "R12", "R21", "R30", "R13", "R22", "R31", "R23", "R32", "R33",
-)
+ORDER = ("F10", "F11", "F20", "F12", "F21", "F30", "F13", "F22", "F31", "F23", "F32", "C0", "F33", "R10", "R11", "C1", "R20", "R21", "R12", "R13", "R30", "R31", "R22", "R23", "R32", "R33",)
 
 
 def exchange_kernel(
@@ -123,23 +120,29 @@
             gather_b[i][s].wait_recv()
             send(gather_c[i][2 + s])
 
-    def compute(i):
-        for s in range(4):
-            gather_c[i][s].wait_recv()
+    def compute(j):
+        pair = (2 * j, 2 * j + 1)
+        for i in pair:
+            for s in range(4):
+                gather_c[i][s].wait_recv()
         if not loaded:
             for load in loads:
                 load.wait()
             loaded.append(True)
-        own, other = rows[i, 0, :, 0:half], rows[i, 1, :, 0:half]
+        count = 4 * tok
+        own = rows[2 * j:2 * j + 2, 0, :, 0:half].reshape(2 * count, half)
+        other = rows[2 * j:2 * j + 2, 1, :, 0:half].reshape(2 * count, half)
         dot = functools.partial(jnp.dot, preferred_element_type=jnp.float32)
         gated = dot(own, w_gate[0]) + dot(other, w_gate[1])
         lifted = dot(own, w_up[0]) + dot(other, w_up[1])
         hidden = (gated / (1.0 + jnp.exp(-gated)) * lifted).astype(jnp.bfloat16)
         away = dot(hidden, w_down[1]).astype(jnp.bfloat16)
-        for s in range(4):
-            part_send[i, swap[s] * tok:(swap[s] + 1) * tok, :] = away[s * tok:(s + 1) * tok]
-        send(reduce_p[i])
-        part_own[i] = dot(hidden, w_down[0]).astype(jnp.bfloat16)
+        for i in pair:
+            for s in range(4):
+                first = (i % 2) * count + s * tok
+                part_send[i, swap[s] * tok:(swap[s] + 1) * tok, :] = away[first:first + tok]
+            send(reduce_p[i])
+        part_own[2 * j:2 * j + 2] = dot(hidden, w_down[0]).astype(jnp.bfloat16).reshape(2, count, half)
 
     def first_sum(i):
         reduce_p[i].wait_recv()

time: 43.7 us -> 42 us (0.961)
  Pallas kernels: 42 us -> 40.3 us
    pallas_call x1, Pallas kernels: 42 us -> 40.3 us  [exchange(): pl.pallas_call(functools.partial(exchange_kernel, owners, layers), out_sh...]
where the time goes in v3:
time: 42 us; the launch traced here: 41.8 us
  Pallas kernels  40.3 us (96%)
  local copies, waits for them, and re-layouts  1.45 us (3%)
    pallas_call x1, Pallas kernels, exchange(): pl.pallas_call(functools.partial(exchange_kernel, owners, layers), out_sh...  40.3 us
    unnamed x1, local copies, waits for them, and re-layouts  1.45 us

profile of v3, /device:TPU:0, one launch (start us, length us, event | category | flops | bytes accessed | tf_op | source)
XLA Modules:
  0.0 41.8 jit_solution(8907757259202719115)
XLA Ops:
  0.0 40.3 %shard_map.64 = bf16[1,16,1792]{2,1,0:T(8,128)(2,1)} custom-call(bf16[1,16,1792]{2,1,0:T(8,128)(2,1)} %tokens_ref.1, s32[1,8,16]{2,1,0:T(8,128)} %bitcast.2, s32[1,8,16]{2,1,0:T(8,128)} %bitcast.3, bf16[1,3584,512]{2,1,0:T(8,128)(2,1)} %gate_ref.1, bf16[1,3584,512]{2,1,0:T(8,128)(2,1)} %up_ref.1, bf16[1,512,3584]{2,1,0:T(8,128)(2,1)} %down_ref.1), custom_call_target="tpu_custom_call" | custom-call | tf_op jit(solution)/shard_map/pallas_call | solution.py:197
  40.3 1.4 %copy.8 = bf16[1,16,1792]{2,1,0:T(8,128)(2,1)} copy(bf16[1,16,1792]{2,1,0:T(8,128)(2,1)} %shard_map.64) | data formatting | bytes 114688

commit v4 on v3

--- a/solution.py
+++ b/solution.py
@@ -8,7 +8,7 @@
 
 MESH = pl.DeviceIdType.MESH
 LANES = 128
-ORDER = ("F10", "F11", "F20", "F12", "F21", "F30", "F13", "F22", "F31", "F23", "F32", "C0", "F33", "R10", "R11", "C1", "R20", "R21", "R12", "R13", "R30", "R31", "R22", "R23", "R32", "R33",)
+ORDER = ("F10", "F11", "F20", "F12", "F21", "F30", "F13", "F22", "F31", "F23", "C0", "F32", "F33", "R11", "R10", "C1", "R12", "R13", "R21", "R20", "R22", "R23", "R31", "R32", "R33", "R30",)
 
 
 def exchange_kernel(

time: 42 us -> 40.3 us (0.960)
  Pallas kernels: 40.3 us -> 38.6 us
    pallas_call x1, Pallas kernels: 40.3 us -> 38.6 us  [exchange(): pl.pallas_call(functools.partial(exchange_kernel, owners, layers), out_sh...]
where the time goes in v4:
time: 40.3 us; the launch traced here: 40.1 us
  Pallas kernels  38.6 us (96%)
  local copies, waits for them, and re-layouts  1.45 us (4%)
    pallas_call x1, Pallas kernels, exchange(): pl.pallas_call(functools.partial(exchange_kernel, owners, layers), out_sh...  38.6 us
    unnamed x1, local copies, waits for them, and re-layouts  1.45 us

profile of v4, /device:TPU:0, one launch (start us, length us, event | category | flops | bytes accessed | tf_op | source)
XLA Modules:
  0.0 40.1 jit_solution(8191154849021981650)
XLA Ops:
  0.0 38.6 %shard_map.64 = bf16[1,16,1792]{2,1,0:T(8,128)(2,1)} custom-call(bf16[1,16,1792]{2,1,0:T(8,128)(2,1)} %tokens_ref.1, s32[1,8,16]{2,1,0:T(8,128)} %bitcast.2, s32[1,8,16]{2,1,0:T(8,128)} %bitcast.3, bf16[1,3584,512]{2,1,0:T(8,128)(2,1)} %gate_ref.1, bf16[1,3584,512]{2,1,0:T(8,128)(2,1)} %up_ref.1, bf16[1,512,3584]{2,1,0:T(8,128)(2,1)} %down_ref.1), custom_call_target="tpu_custom_call" | custom-call | tf_op jit(solution)/shard_map/pallas_call | solution.py:197
  38.7 1.4 %copy.8 = bf16[1,16,1792]{2,1,0:T(8,128)(2,1)} copy(bf16[1,16,1792]{2,1,0:T(8,128)(2,1)} %shard_map.64) | data formatting | bytes 114688
